TPU v7x, 32 devices: a whole 2x2x4 slice. The times are simulated.
32 devices in a mesh: row: 16 (over z, x, core), col: 2 (over y).
Axes of the slice: x: 2, y: 2, z: 4, core: 2. Of those that a mesh axis runs over, the one named last changes fastest.
Arguments:
- features: bfloat16 [16384, 512], P(('row', 'col')), may hold values from -6 to 6
- factor: float32 [16384, 1024], P(('row', 'col')), may hold values from -0.03 to 0.03
- ip_weights: float32 [16384], P(('row', 'col')), may hold values from 0.1 to 30
- pivot_owner: int32 [256], replicated, may hold values from 0 to 31, as said below
- pivot_position: int32 [256], replicated, may hold values from 0 to 511, as said below
Outputs:
- new_columns: float32 [16384, 256], P(('row', 'col'))
- gram_rows: float32 [256, 1280], replicated
Inputs may be any that keep to these rules, and one draw needn't show every extreme that they name: `pivot_owner`: each device owns at most 18 pivots, and some device owns exactly 18. `pivot_position`: pivots with the same owner have different positions.
All inputs are finite; a program needn't handle non-finite values.
Results may differ from a plain program's by a relative error of at most 0.0003.
Values may be sent and summed in bfloat16 or wider, within the bound.
No kernel may reach another device: no remote copies, remote signals or barrier semaphores. Data moves between devices by JAX's collectives and lax.ppermute only.
A program may use at most 64 MiB of HBM per device.

v0:
```python
import jax
import jax.numpy as jnp
from jax import lax
from jax.sharding import PartitionSpec as P

F = 512
kernel_rates = (0.25, 0.5, 1.0)
kernel_mixes = (0.5, 0.3, 0.2)


def kernel_of(left, right):
    cross_term = jnp.dot(left, right.T, preferred_element_type=jnp.float32)
    left_norms = jnp.sum(jnp.square(left.astype(jnp.float32)), axis=1)
    right_norms = jnp.sum(jnp.square(right.astype(jnp.float32)), axis=1)
    distance = left_norms[:, None] + right_norms[None, :] - 2.0 * cross_term
    total = jnp.zeros_like(distance)
    for rate, mixing in zip(kernel_rates, kernel_mixes):
        total = total + mixing * jnp.exp(-(rate / F) * distance)
    return total


def body(features, factor, ip_weights, pivot_owner, pivot_position):
    devices = lax.axis_size("row") * lax.axis_size("col")
    device_rank = lax.axis_index("row") * lax.axis_size("col") + lax.axis_index("col")
    pivot_count = pivot_owner.shape[0]
    slot_count = 2 * pivot_count // devices + 2
    same_owner = pivot_owner[:, None] == pivot_owner[None, :]
    earlier = jnp.arange(pivot_count)[None, :] < jnp.arange(pivot_count)[:, None]
    slot_rank = jnp.sum((same_owner & earlier).astype(jnp.int32), axis=1)
    chosen = (pivot_owner == device_rank)[None, :] & (
        slot_rank[None, :] == jnp.arange(slot_count)[:, None]
    )
    filled = jnp.any(chosen, axis=1)[:, None]
    slot_rows = jnp.sum(jnp.where(chosen, pivot_position[None, :], 0), axis=1)
    slot_x = jnp.where(filled, features[slot_rows], jnp.zeros((), jnp.bfloat16))
    slot_h = jnp.where(filled, factor[slot_rows], 0.0)
    every_x = lax.all_gather(slot_x, ("row", "col"), axis=0, tiled=True)
    every_h = lax.all_gather(slot_h, ("row", "col"), axis=0, tiled=True)
    source = pivot_owner * slot_count + slot_rank
    pivot_x = every_x[source]
    pivot_h = every_h[source]
    residual = kernel_of(features, pivot_x) - jnp.dot(
        factor, pivot_h.T, precision=lax.Precision.HIGHEST
    )
    block = kernel_of(pivot_x, pivot_x) - jnp.dot(
        pivot_h, pivot_h.T, precision=lax.Precision.HIGHEST
    )
    lower_block = jnp.linalg.cholesky(block)
    new_columns = jax.scipy.linalg.solve_triangular(lower_block, residual.T, lower=True).T
    weighted = new_columns * ip_weights[:, None]
    left_part = jnp.dot(weighted.T, factor, precision=lax.Precision.HIGHEST)
    right_part = jnp.dot(weighted.T, new_columns, precision=lax.Precision.HIGHEST)
    local_gram = jnp.concatenate([left_part, right_part], axis=1)
    summed = lax.psum(local_gram, ("row", "col"))
    total_samples = features.shape[0] * devices
    return (new_columns, summed / total_samples)


def solution(mesh):
    placed = (P(("row", "col"), None), P(("row", "col"), None), P(("row", "col")), P(), P())
    return jax.shard_map(
        body, mesh=mesh, in_specs=placed, out_specs=(P(("row", "col"), None), P()), check_vma=False
    )
```

profile of v0, /device:TPU:0, one launch (start us, length us, event | category | flops | bytes accessed | tf_op | source)
XLA Modules:
  0.0 309.8 jit_solution(2607362890105495387)
XLA Ops:
  7.2 0.0 all-gather.4.cloned.1.call-start
  7.2 1.0 convert_reduce_fusion
  8.3 0.7 broadcast_compare_fusion
  8.9 0.1 fusion.21
  9.1 0.8 select_reduce_fusion.2
  9.9 0.6 gather_fusion.2
  10.5 0.7 select_bitcast_fusion
  11.2 0.0 all-gather.4.cloned.1.call-update
  11.2 0.0 all-reduce.3.cloned.1.call-start
  11.3 1.7 gather_fusion
  13.0 0.1 select_bitcast_fusion.2
  13.1 75.1 %all-gather = bf16[32,18,512]{2,1,0:T(8,128)(2,1)S(1)} all-gather(bf16[1,18,512]{2,1,0:T(8,128)(2,1)S(1)} %select_bitcast_fusion.2), channel_id=1, replica_groups=mesh['row'=16,'col'=2] {'row','col'}, dimensions={0}, use_global_device_ids=true | all-gather | bytes 608256 | tf_op jit(solution)/shard_map/all_gather | solution.py:37
  88.1 0.2 reshape.100
  88.4 1.2 gather_fusion.1
  89.5 0.3 convolution_multiply_fusion.1
  89.8 0.8 copy.23
  90.6 0.1 multiply_reduce_fusion.1
  90.8 0.2 multiply_reduce_fusion
  91.0 1.1 fusion
  92.1 3.1 reshape.102
  95.2 3.2 %gather_fusion.3 = f32[256,1024]{1,0:T(8,128)S(1)} fusion(f32[576,1024]{1,0:T(8,128)} %reshape.102, s32[1024]{0:T(1024)S(1)} %pad_clamp_fusion), kind=kCustom, calls=%fused_computation.3 | custom fusion | bytes 2098176 | tf_op jit(solution)/shard_map/gather | solution.py:41
  98.4 1.7 fusion.26
  100.1 2.9 convolution_subtract_fusion
  103.0 1.1 copy.24
  104.1 1.5 fusion.9
  105.6 11.7 %cholesky.50 = f32[128,128]{1,0:T(8,128)S(1)} custom-call(f32[128,128]{1,0:T(8,128)S(1)} %cholesky.118), custom_call_target="Cholesky" | custom-call | tf_op jit(solution)/shard_map/jit(cholesky)/cholesky | solution.py:48
  117.4 9.8 %custom-call.15 = f32[1,128,128]{1,2,0:T(8,128)S(1)} custom-call(f32[1,128,128]{2,1,0:T(8,128)S(1)} %get-tuple-element.31), custom_call_target="InvertDiagBlocksLowerTriangular" | custom-call | tf_op jit(solution)/shard_map/jit(cholesky)/cholesky | solution.py:48
  127.2 0.2 constant_dynamic-update-slice_fusion.1
  127.4 0.3 convolution_subtract_fusion.2
  127.7 11.9 %cholesky.105 = f32[128,128]{1,0:T(8,128)S(1)} custom-call(f32[128,128]{1,0:T(8,128)S(1)} %convolution_subtract_fusion.2), custom_call_target="Cholesky" | custom-call | tf_op jit(solution)/shard_map/jit(cholesky)/cholesky | solution.py:48
  139.6 0.7 compare_reduce_fusion
  141.7 0.1 triangular_solve.60
  141.8 5.3 %while.1 = (s32[]{:T(128)}, f32[256,256]{1,0:T(8,128)S(1)}, s32[2,2]{1,0:T(2,128)S(1)}, f32[2,128,128]{2,1,0:T(8,128)}, s32[]{:T(128)}) while((s32[]{:T(128)}, f32[256,256]{1,0:T(8,128)S(1)}, s32[2,2]{1,0:T(2,128)S(1)}, f32[2,128,128]{2,1,0:T(8,128)}, s32[]{:T(128)}) %tuple.31), condition=%wide.while_cond, body=%wide.while_body.sunk | while | flops 2 | bytes 132205 | solution.py:49
  141.8 0.6 fusion.41
  142.4 2.0 bitcast_dynamic-update-slice_fusion.2
  144.5 0.6 fusion.41
  145.1 2.0 bitcast_dynamic-update-slice_fusion.2
  147.1 20.5 %custom-call.16 = f32[2,128,128]{1,2,0:T(8,128)S(1)} custom-call(f32[2,128,128]{2,1,0:T(8,128)} %get-tuple-element.9), custom_call_target="InvertDiagBlocksLowerTriangular" | custom-call | tf_op jit(solution)/shard_map/jit(_solve_triangular)/triangular_solve | solution.py:49
  167.6 0.4 fusion.6
  168.0 0.4 convolution_subtract_fusion.1
  168.4 0.4 fusion.16
  168.9 0.6 fusion.1
  169.5 1.9 fusion.3
  171.4 1.2 pad_maximum_fusion
  172.5 0.0 all-reduce.3.cloned.1.call-update
  172.6 1.0 copy.26
  173.6 126.9 %all-reduce.3.cloned.1.call-done = f32[256,1280]{1,0:T(8,128)} async-done(((f32[256,1280]{1,0:T(8,128)}), f32[256,1280]{1,0:T(8,128)}) %all-reduce.3.cloned.1.call-update) | async-done | bytes 1310736 | tf_op jit(solution)/shard_map/psum | solution.py:54
  300.5 2.5 broadcast_multiply_fusion
  (31 shorter events, 0.3 us)
Async XLA Ops:
  7.2 2.7 copy-start
  7.2 81.2 %copy-start.6 = (s32[256]{0:T(256)S(1)}, s32[256]{0:T(256)}, u32[]{:S(2)}) copy-start(s32[256]{0:T(256)} %param.8) | copy-start | bytes 3076
  7.2 84.9 %all-gather.4.cloned.1.call-start = ((), (), s32[]{:S(2)}) async-start(), calls=%async_computation.1 | async-start | bytes 3244032 | tf_op jit(solution)/shard_map/all_gather | solution.py:38
  11.2 289.3 %all-reduce.3.cloned.1.call-start = ((), (), s32[]{:S(2)}) async-start(), calls=%async_computation | async-start | bytes 2621440 | tf_op jit(solution)/shard_map/psum | solution.py:54
  88.3 2.5 copy-start.1
  89.8 2.3 copy-start.2
  98.4 1.7 copy-start.5
  100.1 4.0 %copy-start.3 = (f32[256,256]{0,1:T(8,128)S(1)}, f32[256,256]{0,1:T(8,128)}, u32[]{:S(2)}) copy-start(f32[256,256]{0,1:T(8,128)} %copy-done.2) | copy-start | bytes 786436
  104.1 63.5 %copy-start.4 = (f32[256,512]{1,0:T(8,128)S(1)}, f32[256,512]{1,0:T(8,128)}, u32[]{:S(2)}) copy-start(f32[256,512]{1,0:T(8,128)} %convolution_subtract_fusion) | copy-start | bytes 1572868
  117.4 51.5 %copy-start.7 = (f32[512]{0:T(512)S(1)}, f32[512]{0:T(512)}, u32[]{:S(2)}) copy-start(f32[512]{0:T(512)} %param.7) | copy-start | bytes 6148
Sparse Core Ops, SparseCore 0:
  11.5 63.7 all-gather.3
  172.7 127.7 all-reduce.2
where the time goes:
time: 310 us
  waiting for transfers between devices  127 us (41%)
  blocking collectives  75.1 us (24%)
  other arithmetic  63.6 us (21%)
  local copies, waits for them, and re-layouts  18.3 us (6%)
  between operations  15.7 us (5%)
  matrix products  10.2 us (3%)
    psum x1, waiting for transfers between devices, body(): summed = lax.psum(local_gram, ('row', 'col'))  127 us
    all_gather x1, blocking collectives, body(): every_x = lax.all_gather(slot_x, ('row', 'col'), axis=0, tiled=True)  75.1 us
    another operation x6, other arithmetic, body(): lower_block = jnp.linalg.cholesky(block)  34.2 us
    another operation x3, other arithmetic, body(): jax.scipy.linalg.solve_triangular(lower_block, residual.T, lower=True)  20.5 us
  transfers between devices with their start and end apart: 2, of which 1 were waited for; matrix products, arithmetic and copies ran while one was open for 2% of the time, Pallas kernels for 0%

commit v1 on v0

--- a/solution.py
+++ b/solution.py
@@ -51,7 +51,7 @@
     left_part = jnp.dot(weighted.T, factor, precision=lax.Precision.HIGHEST)
     right_part = jnp.dot(weighted.T, new_columns, precision=lax.Precision.HIGHEST)
     local_gram = jnp.concatenate([left_part, right_part], axis=1)
-    summed = lax.psum(local_gram, ("row", "col"))
+    summed = lax.psum(lax.psum(local_gram, "col"), "row")
     total_samples = features.shape[0] * devices
     return (new_columns, summed / total_samples)
 

time: 310 us -> 321 us (1.035)
  waiting for transfers between devices: 127 us -> 138 us
    psum x1 -> x2, waiting for transfers between devices: 127 us -> 138 us  [body(): summed = lax.psum(lax.psum(local_gram, 'col'), 'row')]
  transfers between devices with their start and end apart: 2 -> 3, of which waited for: 1 -> 2; matrix products, arithmetic and copies ran while one was open for 2% -> 2% of each run, Pallas kernels for 0% -> 0%
where the time goes in v1:
time: 321 us
  waiting for transfers between devices  138 us (43%)
  blocking collectives  75.1 us (23%)
  other arithmetic  63.6 us (20%)
  local copies, waits for them, and re-layouts  18.3 us (6%)
  between operations  15.4 us (5%)
  matrix products  10.2 us (3%)
    psum x2, waiting for transfers between devices, body(): summed = lax.psum(lax.psum(local_gram, 'col'), 'row')  138 us
    all_gather x1, blocking collectives, body(): every_x = lax.all_gather(slot_x, ('row', 'col'), axis=0, tiled=True)  75.1 us
    another operation x6, other arithmetic, body(): lower_block = jnp.linalg.cholesky(block)  34.2 us
    another operation x3, other arithmetic, body(): jax.scipy.linalg.solve_triangular(lower_block, residual.T, lower=True)  20.5 us
  transfers between devices with their start and end apart: 3, of which 2 were waited for; matrix products, arithmetic and copies ran while one was open for 2% of the time, Pallas kernels for 0%

profile of v1, /device:TPU:0, one launch (start us, length us, event | category | flops | bytes accessed | tf_op | source)
XLA Modules:
  0.0 321.0 jit_solution(2771996350621624352)
XLA Ops:
  7.2 0.0 all-gather.4.cloned.1.call-start
  7.2 1.0 convert_reduce_fusion
  8.3 0.7 broadcast_compare_fusion
  8.9 0.1 fusion.21
  9.1 0.8 select_reduce_fusion.2
  9.9 0.6 gather_fusion.2
  10.5 0.7 select_bitcast_fusion
  11.2 0.0 all-reduce.4.cloned.1.call-start
  11.3 1.7 gather_fusion
  13.0 0.1 select_bitcast_fusion.2
  13.1 75.1 %all-gather = bf16[32,18,512]{2,1,0:T(8,128)(2,1)S(1)} all-gather(bf16[1,18,512]{2,1,0:T(8,128)(2,1)S(1)} %select_bitcast_fusion.2), channel_id=1, replica_groups=mesh['row'=16,'col'=2] {'row','col'}, dimensions={0}, use_global_device_ids=true | all-gather | bytes 608256 | tf_op jit(solution)/shard_map/all_gather | solution.py:37
  88.1 0.2 reshape.100
  88.4 1.2 gather_fusion.1
  89.5 0.3 convolution_multiply_fusion.1
  89.8 0.8 copy.23
  90.6 0.1 multiply_reduce_fusion.1
  90.8 0.2 multiply_reduce_fusion
  91.0 1.1 fusion
  92.1 3.1 reshape.102
  95.2 3.2 %gather_fusion.3 = f32[256,1024]{1,0:T(8,128)S(1)} fusion(f32[576,1024]{1,0:T(8,128)} %reshape.102, s32[1024]{0:T(1024)S(1)} %pad_clamp_fusion), kind=kCustom, calls=%fused_computation.3 | custom fusion | bytes 2098176 | tf_op jit(solution)/shard_map/gather | solution.py:41
  98.4 1.7 fusion.26
  100.1 2.9 convolution_subtract_fusion
  103.0 1.1 copy.24
  104.1 1.5 fusion.9
  105.6 11.7 %cholesky.50 = f32[128,128]{1,0:T(8,128)S(1)} custom-call(f32[128,128]{1,0:T(8,128)S(1)} %cholesky.118), custom_call_target="Cholesky" | custom-call | tf_op jit(solution)/shard_map/jit(cholesky)/cholesky | solution.py:48
  117.4 9.8 %custom-call.15 = f32[1,128,128]{1,2,0:T(8,128)S(1)} custom-call(f32[1,128,128]{2,1,0:T(8,128)S(1)} %get-tuple-element.31), custom_call_target="InvertDiagBlocksLowerTriangular" | custom-call | tf_op jit(solution)/shard_map/jit(cholesky)/cholesky | solution.py:48
  127.2 0.2 constant_dynamic-update-slice_fusion.1
  127.4 0.3 convolution_subtract_fusion.2
  127.7 11.9 %cholesky.105 = f32[128,128]{1,0:T(8,128)S(1)} custom-call(f32[128,128]{1,0:T(8,128)S(1)} %convolution_subtract_fusion.2), custom_call_target="Cholesky" | custom-call | tf_op jit(solution)/shard_map/jit(cholesky)/cholesky | solution.py:48
  139.6 0.7 compare_reduce_fusion
  141.7 0.1 triangular_solve.60
  141.8 5.3 %while.1 = (s32[]{:T(128)}, f32[256,256]{1,0:T(8,128)S(1)}, s32[2,2]{1,0:T(2,128)S(1)}, f32[2,128,128]{2,1,0:T(8,128)}, s32[]{:T(128)}) while((s32[]{:T(128)}, f32[256,256]{1,0:T(8,128)S(1)}, s32[2,2]{1,0:T(2,128)S(1)}, f32[2,128,128]{2,1,0:T(8,128)}, s32[]{:T(128)}) %tuple.31), condition=%wide.while_cond, body=%wide.while_body.sunk | while | flops 2 | bytes 132205 | solution.py:49
  141.8 0.6 fusion.41
  142.4 2.0 bitcast_dynamic-update-slice_fusion.2
  144.5 0.6 fusion.41
  145.1 2.0 bitcast_dynamic-update-slice_fusion.2
  147.1 20.5 %custom-call.16 = f32[2,128,128]{1,2,0:T(8,128)S(1)} custom-call(f32[2,128,128]{2,1,0:T(8,128)} %get-tuple-element.9), custom_call_target="InvertDiagBlocksLowerTriangular" | custom-call | tf_op jit(solution)/shard_map/jit(_solve_triangular)/triangular_solve | solution.py:49
  167.6 0.4 fusion.6
  168.0 0.4 convolution_subtract_fusion.1
  168.4 0.4 fusion.16
  168.9 0.6 fusion.1
  169.5 1.9 fusion.3
  171.4 1.2 pad_maximum_fusion
  172.6 0.0 all-reduce.6.cloned.1.call-start
  172.6 41.8 %all-reduce.4.cloned.1.call-done = f32[256,1280]{1,0:T(8,128)} async-done(((f32[256,1280]{1,0:T(8,128)}), f32[256,1280]{1,0:T(8,128)}) %all-reduce.4.cloned.1.call-update) | async-done | bytes 1310736 | tf_op jit(solution)/shard_map/psum | solution.py:54
  214.5 1.0 copy.26
  215.5 96.6 %all-reduce.6.cloned.1.call-done = f32[256,1280]{1,0:T(8,128)} async-done(((f32[256,1280]{1,0:T(8,128)}), f32[256,1280]{1,0:T(8,128)}) %all-reduce.6.cloned.1.call-update) | async-done | bytes 1310736 | tf_op jit(solution)/shard_map/psum | solution.py:54
  312.1 2.5 broadcast_multiply_fusion
  (34 shorter events, 0.3 us)
Async XLA Ops:
  7.2 2.7 copy-start
  7.2 81.2 %copy-start.6 = (s32[256]{0:T(256)S(1)}, s32[256]{0:T(256)}, u32[]{:S(2)}) copy-start(s32[256]{0:T(256)} %param.8) | copy-start | bytes 3076
  7.2 84.9 %all-gather.4.cloned.1.call-start = ((), (), s32[]{:S(2)}) async-start(), calls=%async_computation.2 | async-start | bytes 3244032 | tf_op jit(solution)/shard_map/all_gather | solution.py:38
  11.2 203.2 %all-reduce.4.cloned.1.call-start = ((), (), s32[]{:S(2)}) async-start(), calls=%async_computation | async-start | bytes 2621440 | tf_op jit(solution)/shard_map/psum | solution.py:54
  88.3 2.5 copy-start.1
  89.8 2.3 copy-start.2
  98.4 1.7 copy-start.5
  100.1 4.0 %copy-start.3 = (f32[256,256]{0,1:T(8,128)S(1)}, f32[256,256]{0,1:T(8,128)}, u32[]{:S(2)}) copy-start(f32[256,256]{0,1:T(8,128)} %copy-done.2) | copy-start | bytes 786436
  104.1 63.5 %copy-start.4 = (f32[256,512]{1,0:T(8,128)S(1)}, f32[256,512]{1,0:T(8,128)}, u32[]{:S(2)}) copy-start(f32[256,512]{1,0:T(8,128)} %convolution_subtract_fusion) | copy-start | bytes 1572868
  117.4 51.5 %copy-start.7 = (f32[512]{0:T(512)S(1)}, f32[512]{0:T(512)}, u32[]{:S(2)}) copy-start(f32[512]{0:T(512)} %param.7) | copy-start | bytes 6148
  172.6 139.5 %all-reduce.6.cloned.1.call-start = ((), (), s32[]{:S(2)}) async-start(), calls=%async_computation.1 | async-start | bytes 2621440 | tf_op jit(solution)/shard_map/psum | solution.py:54
Sparse Core Ops, SparseCore 0:
  11.5 63.7 all-gather.3
  172.7 41.6 all-reduce.3
  217.9 94.1 all-reduce.5
